TPU v7x, 32 devices: a whole 2x2x4 slice. The times are simulated.
32 devices in a mesh: seq: 16 (over z, x, core), chan: 2 (over y).
Axes of the slice: x: 2, y: 2, z: 4, core: 2. Of those that a mesh axis runs over, the one named last changes fastest.
Arguments:
- step_size: bfloat16 [2, 5120, 2048], P(None, ('chan', 'seq')), as said below
- inputs: bfloat16 [2, 5120, 2048], P(None, ('chan', 'seq')), may hold values from -6 to 6
- gate_input: bfloat16 [2, 5120, 2048], P(None, ('chan', 'seq')), may hold values from -6 to 6
- decay_rate: float32 [5120], P('chan'), as said below
- norm_gain: float32 [5120], P('chan'), may hold values from 0.1 to 1.9
- resets: int32 [2, 8], replicated, may hold values from 1 to 2047
Outputs:
- normed: bfloat16 [2, 5120, 2048], P(None, 'chan', 'seq')
Inputs may be any that keep to these rules, and one draw needn't show every extreme that they name: `step_size`: positive step sizes. `decay_rate`: positive rates. `resets`: positions within the sequence; several may coincide.
All inputs are finite; a program needn't handle non-finite values.
Results may differ from a plain program's by a relative error of at most 0.001.
Values may be sent and summed in bfloat16 or wider, within the bound.
A program may use at most 64 MiB of HBM per device.

v0:
```python
import math
import jax
import jax.numpy as jnp
from jax import lax
from jax.sharding import PartitionSpec as P

FEATURE_WIDTH = 5120


def compose(earlier, later):
    return (earlier[0] * later[0], later[0] * earlier[1] + later[1])


def coefficients(steps, values, rates):
    scaled = steps.astype(jnp.float32) * rates[None, :, None]
    drive = jnp.sqrt(-jnp.expm1(-2.0 * scaled)) * values.astype(jnp.float32)
    return (scaled, drive)


def marks_for(resets, places):
    return jnp.any(resets[:, :, None] == places[None, None, :], axis=1)


def local_scan(scaled, drive, marks):
    rows, chans, length = scaled.shape
    places = jnp.arange(length, dtype=jnp.int32)
    upper = (places[:, None] <= places[None, :]).astype(jnp.float32)
    cumul = jnp.einsum("rck,ku->rcu", scaled, upper, precision=lax.Precision.HIGHEST)
    counts = jnp.dot(marks.astype(jnp.float32), upper, precision=lax.Precision.HIGHEST)
    linked = (counts[:, :, None] == counts[:, None, :]) & (places[:, None] >= places[None, :])[None]
    group = math.gcd(chans, 64)

    def one_group(pieces):
        cumul_part, drive_part = pieces
        spread = cumul_part[:, :, :, None] - cumul_part[:, :, None, :]
        weight = jnp.where(linked[:, None], jnp.exp(-jnp.maximum(spread, 0.0)), jnp.float32(0.0))
        return jnp.einsum("rctj,rcj->rct", weight, drive_part, precision=lax.Precision.HIGHEST)

    def split_groups(array):
        return jnp.moveaxis(array.reshape(rows, chans // group, group, length), 1, 0)

    results = lax.map(one_group, (split_groups(cumul), split_groups(drive)))
    local_state = jnp.moveaxis(results, 0, 1).reshape(rows, chans, length)
    running = jnp.where(counts[:, None, :] == 0.0, jnp.exp(-cumul), jnp.float32(0.0))
    return (running, local_state)


def finish(gated, norm_gain):
    squares = jnp.sum(gated * gated, axis=1)
    total = lax.psum(squares, "chan")
    mean_square = total / jnp.float32(FEATURE_WIDTH)
    scale_rows = lax.rsqrt(mean_square + 1e-05)
    return (gated * scale_rows[:, None, :] * norm_gain[None, :, None]).astype(jnp.bfloat16)


def per_device(step_size, inputs, gate_input, decay_rate, norm_gain, resets):
    position = lax.axis_index("seq")
    batch, width, length = step_size.shape
    rates = lax.dynamic_slice_in_dim(decay_rate, position * width, width)
    places = jnp.arange(length, dtype=jnp.int32)
    scaled, drive = coefficients(step_size, inputs, rates)
    marks = marks_for(resets, places)
    piece = math.gcd(length, 128)
    count_blocks = length // piece

    def to_blocks(array):
        moved = jnp.moveaxis(array.reshape(batch, width, count_blocks, piece), 2, 1)
        return moved.reshape(batch * count_blocks, width, piece)

    running, local_state = local_scan(
        to_blocks(scaled), to_blocks(drive), marks.reshape(batch * count_blocks, piece)
    )
    total_decay = running[:, :, -1].reshape(batch, count_blocks, width)
    total_state = local_state[:, :, -1].reshape(batch, count_blocks, width)
    prefix = lax.associative_scan(compose, (total_decay, total_state), axis=1)
    incoming = jnp.concatenate(
        [jnp.zeros((batch, 1, width), jnp.float32), prefix[1][:, :-1]], axis=1
    )
    blocked = local_state + running * incoming.reshape(batch * count_blocks, width)[:, :, None]
    state = jnp.moveaxis(blocked.reshape(batch, count_blocks, width, piece), 1, 2).reshape(
        batch, width, length
    )
    local_gated = state * jax.nn.silu(gate_input.astype(jnp.float32))
    gated = lax.all_to_all(local_gated, "seq", split_axis=2, concat_axis=1, tiled=True)
    return finish(gated, norm_gain)


def solution(mesh):
    in_specs = (
        P(None, ("chan", "seq"), None),
        P(None, ("chan", "seq"), None),
        P(None, ("chan", "seq"), None),
        P("chan"),
        P("chan"),
        P(),
    )
    out_specs = P(None, "chan", "seq")
    return jax.shard_map(
        per_device, mesh=mesh, in_specs=in_specs, out_specs=out_specs, check_vma=False
    )
```

profile of v0, /device:TPU:0, one launch (start us, length us, event | category | flops | bytes accessed | tf_op | source)
XLA Modules:
  0.0 738.9 jit_solution(2449741942070967262)
XLA Ops:
  0.0 0.8 dynamic_slice.10
  0.8 5.1 convert_multiply_fusion.1
  5.9 0.5 copy.63
  6.4 0.2 bitcast_bitcast_fusion.1
  6.6 0.0 copy-start.4
  6.6 0.8 copy.51
  7.4 0.0 copy-done.4
  7.4 0.1 fusion.19
  7.5 0.1 broadcast_compare_fusion
  7.7 2.9 exponential_select_fusion
  10.6 0.0 copy-start.2
  10.6 0.2 copy.68
  10.8 1.5 copy-done.2
  12.3 0.5 copy.64
  12.8 0.2 bitcast_bitcast_fusion
  13.0 2.3 copy.53
  15.3 581.5 %while.11 = (s32[]{:T(128)}, f32[5,32,32,128]{3,2,1,0:T(8,128)}, f32[5,32,32,128]{3,2,1,0:T(8,128)S(1)}, f32[5,32,32,128]{3,2,0,1:T(8,128)}, f32[32,128]{1,0:T(8...) while((s32[]{:T(128)}, f32[5,32,32,128]{3,2,1,0:T(8,128)}, f32[5,32,32,128]{3,2,1,0:T(8,128)S(1)}, ...), condition=%wide.region_2.3_spmd.clone, body=%wide.region_1.2_spmd.clone.sunk | while | flops 269484032 | bytes 5800533 | solution.py:42
  29.8 1.1 constant_dynamic-slice_fusion.2
  30.9 0.7 compare_and_fusion.2
  31.6 110.7 %fusion.44 = f32[32,32,1,128]{3,2,1,0:T(1,128)S(1)} fusion(f32[32,32,128,1]{2,3,1,0:T(1,128)S(1)} %bitcast.83, f32[32,32,128]{2,1,0:T(8,128)S(1)} %dynamic-slice_bitcast_fusion.2, pred[32,128,128]{2,1,0:T(8,128)(4,1)S(1)} %compare_and_fusion.2), kind=kOutput, calls=%fused_computation.1.clone.2 | convolution fusion | flops 268435456 | bytes 2097152 | tf_op jit(solution)/shard_map/while/body/eval_jaxpr/rctj,rcj->rct/dot_general | solution.py:37
  142.3 0.9 constant_dynamic-update-slice_fusion.2
  143.2 1.1 constant_dynamic-slice_fusion.2
  144.3 0.7 compare_and_fusion.2
  145.0 110.7 %fusion.44 = f32[32,32,1,128]{3,2,1,0:T(1,128)S(1)} fusion(f32[32,32,128,1]{2,3,1,0:T(1,128)S(1)} %bitcast.83, f32[32,32,128]{2,1,0:T(8,128)S(1)} %dynamic-slice_bitcast_fusion.2, pred[32,128,128]{2,1,0:T(8,128)(4,1)S(1)} %compare_and_fusion.2), kind=kOutput, calls=%fused_computation.1.clone.2 | convolution fusion | flops 268435456 | bytes 2097152 | tf_op jit(solution)/shard_map/while/body/eval_jaxpr/rctj,rcj->rct/dot_general | solution.py:37
  255.7 0.9 constant_dynamic-update-slice_fusion.2
  256.6 1.1 constant_dynamic-slice_fusion.2
  257.7 0.7 compare_and_fusion.2
  258.5 110.7 %fusion.44 = f32[32,32,1,128]{3,2,1,0:T(1,128)S(1)} fusion(f32[32,32,128,1]{2,3,1,0:T(1,128)S(1)} %bitcast.83, f32[32,32,128]{2,1,0:T(8,128)S(1)} %dynamic-slice_bitcast_fusion.2, pred[32,128,128]{2,1,0:T(8,128)(4,1)S(1)} %compare_and_fusion.2), kind=kOutput, calls=%fused_computation.1.clone.2 | convolution fusion | flops 268435456 | bytes 2097152 | tf_op jit(solution)/shard_map/while/body/eval_jaxpr/rctj,rcj->rct/dot_general | solution.py:37
  369.2 0.9 constant_dynamic-update-slice_fusion.2
  370.0 1.1 constant_dynamic-slice_fusion.2
  371.1 0.7 compare_and_fusion.2
  371.9 110.7 %fusion.44 = f32[32,32,1,128]{3,2,1,0:T(1,128)S(1)} fusion(f32[32,32,128,1]{2,3,1,0:T(1,128)S(1)} %bitcast.83, f32[32,32,128]{2,1,0:T(8,128)S(1)} %dynamic-slice_bitcast_fusion.2, pred[32,128,128]{2,1,0:T(8,128)(4,1)S(1)} %compare_and_fusion.2), kind=kOutput, calls=%fused_computation.1.clone.2 | convolution fusion | flops 268435456 | bytes 2097152 | tf_op jit(solution)/shard_map/while/body/eval_jaxpr/rctj,rcj->rct/dot_general | solution.py:37
  482.6 0.9 constant_dynamic-update-slice_fusion.2
  483.4 1.1 constant_dynamic-slice_fusion.2
  484.6 0.7 compare_and_fusion.2
  485.3 110.7 %fusion.44 = f32[32,32,1,128]{3,2,1,0:T(1,128)S(1)} fusion(f32[32,32,128,1]{2,3,1,0:T(1,128)S(1)} %bitcast.83, f32[32,32,128]{2,1,0:T(8,128)S(1)} %dynamic-slice_bitcast_fusion.2, pred[32,128,128]{2,1,0:T(8,128)(4,1)S(1)} %compare_and_fusion.2), kind=kOutput, calls=%fused_computation.1.clone.2 | convolution fusion | flops 268435456 | bytes 2097152 | tf_op jit(solution)/shard_map/while/body/eval_jaxpr/rctj,rcj->rct/dot_general | solution.py:37
  596.0 0.8 constant_dynamic-update-slice_fusion.2
  596.8 2.0 copy.55
  598.8 0.0 copy-start.1
  598.8 0.0 copy-start
  598.8 1.5 copy-done.1
  600.3 1.9 slice_reduce_fusion.1
  602.2 0.0 copy-done
  602.2 1.9 slice_reduce_fusion
  604.8 2.2 multiply_add_fusion
  607.0 3.0 copy.67
  610.0 2.6 reshape.57
  612.6 3.5 fusion.16
  616.1 6.8 copy.57
  622.9 99.6 %all_to_all.18 = f32[2,160,2048]{1,0,2:T(2,128)} all-to-all(f32[2,160,2048]{1,0,2:T(2,128)} %copy.57), channel_id=1, replica_groups=mesh['seq'=16,'chan'=2] {'seq'}, dimensions={2} | all-to-all | bytes 5242880 | tf_op jit(solution)/shard_map/all_to_all | solution.py:84
  722.5 5.3 copy.58
  727.8 0.0 copy-start.3
  727.8 4.2 multiply_reduce_fusion
  732.0 0.1 copy.59
  732.0 5.0 psum.7
  737.0 0.0 copy-done.3
  737.0 1.5 fusion.18
  (48 shorter events, 0.9 us)
Async XLA Ops:
  6.6 0.8 copy-start.4
  10.6 1.7 copy-start.2
  598.8 1.5 copy-start.1
  598.8 3.4 copy-start
  727.8 9.2 %copy-start.3 = (f32[2560]{0:T(1024)S(1)}, f32[2560]{0:T(1024)}, u32[]{:S(2)}) copy-start(f32[2560]{0:T(1024)} %param.12) | copy-start | bytes 30724
where the time goes:
time: 745 us; the launch traced here: 739 us
  matrix products  556 us (75%)
  blocking collectives  105 us (14%)
  local copies, waits for them, and re-layouts  42.4 us (6%)
  other arithmetic  20.3 us (3%)
  loops' own time  14.5 us (2%)
    dot_general x5, matrix products, one_group(): jnp.einsum('rctj,rcj->rct', weight, drive_part, precision=lax.Precision.H...  553 us
    all_to_all x1, blocking collectives, per_device(): lax.all_to_all(local_gated, 'seq', split_axis=2, concat_axis=1, tiled=True)  99.6 us

commit v1 on v0

--- a/solution.py
+++ b/solution.py
@@ -81,7 +81,12 @@
         batch, width, length
     )
     local_gated = state * jax.nn.silu(gate_input.astype(jnp.float32))
-    gated = lax.all_to_all(local_gated, "seq", split_axis=2, concat_axis=1, tiled=True)
+    gated = jnp.concatenate(
+        lax.all_to_all(
+            jnp.stack(jnp.split(local_gated, lax.axis_size("seq"), axis=2)), "seq", 0, 0
+        ),
+        axis=1,
+    )
     return finish(gated, norm_gain)
 
 

time: 745 us -> 667 us (0.90)
  blocking collectives: 105 us -> 70.5 us
  local copies, waits for them, and re-layouts: 42.4 us -> 25.2 us
  loops' own time: 14.5 us -> 0.1 us
    all_to_all x1, blocking collectives: 99.6 us -> 65.6 us  [per_device(): lax.all_to_all(jnp.stack(jnp.split(local_gated, lax.axis_size('seq'), axi...]
    another operation x1, loops' own time: 14.5 us -> 0.1 us  [local_scan(): results = lax.map(one_group, (split_groups(cumul), split_groups(drive)))]
where the time goes in v1:
time: 667 us; the launch traced here: 666 us
  matrix products  556 us (83%)
  blocking collectives  70.5 us (11%)
  local copies, waits for them, and re-layouts  25.2 us (4%)
  other arithmetic  13.7 us (2%)
    dot_general x5, matrix products, one_group(): jnp.einsum('rctj,rcj->rct', weight, drive_part, precision=lax.Precision.H...  553 us
    all_to_all x1, blocking collectives, per_device(): lax.all_to_all(jnp.stack(jnp.split(local_gated, lax.axis_size('seq'), axi...  65.6 us

profile of v1, /device:TPU:0, one launch (start us, length us, event | category | flops | bytes accessed | tf_op | source)
XLA Modules:
  0.0 666.4 jit_solution(189833215169826504)
XLA Ops:
  0.0 0.8 dynamic_slice.10
  0.8 5.1 convert_multiply_fusion.1
  5.9 0.5 copy.36
  6.4 0.2 bitcast_bitcast_fusion.1
  6.6 0.0 copy-start.5
  6.6 0.8 copy.25
  7.4 0.0 copy-done.5
  7.4 0.1 fusion.35
  7.5 0.1 broadcast_compare_fusion
  7.7 2.9 exponential_select_fusion
  10.6 0.0 copy-start.2
  10.6 0.2 copy.40
  10.8 1.5 copy-done.2
  12.3 0.5 copy.37
  12.8 0.2 bitcast_bitcast_fusion
  13.0 2.3 copy.27
  15.3 567.1 %while.11 = (s32[]{:T(128)}, f32[5,32,32,128]{3,2,1,0:T(8,128)}, f32[5,32,32,128]{3,2,1,0:T(8,128)S(1)}, f32[5,32,32,128]{3,2,0,1:T(8,128)}, f32[32,128]{1,0:T(8...) while((s32[]{:T(128)}, f32[5,32,32,128]{3,2,1,0:T(8,128)}, f32[5,32,32,128]{3,2,1,0:T(8,128)S(1)}, ...), condition=%wide.region_2.3_spmd.clone, body=%wide.region_1.2_spmd.clone.sunk | while | flops 269484032 | bytes 5800533 | solution.py:42
  15.3 1.1 constant_dynamic-slice_fusion.2
  16.5 0.7 compare_and_fusion.2
  17.2 110.7 %fusion.60 = f32[32,32,1,128]{3,2,1,0:T(1,128)S(1)} fusion(f32[32,32,128,1]{2,3,1,0:T(1,128)S(1)} %bitcast.145, f32[32,32,128]{2,1,0:T(8,128)S(1)} %dynamic-slice_bitcast_fusion.2, pred[32,128,128]{2,1,0:T(8,128)(4,1)S(1)} %compare_and_fusion.2), kind=kOutput, calls=%fused_computation.1.clone.2 | convolution fusion | flops 268435456 | bytes 2097152 | tf_op jit(solution)/shard_map/while/body/eval_jaxpr/rctj,rcj->rct/dot_general | solution.py:37
  127.9 0.9 constant_dynamic-update-slice_fusion.2
  128.7 1.1 constant_dynamic-slice_fusion.2
  129.9 0.7 compare_and_fusion.2
  130.6 110.7 %fusion.60 = f32[32,32,1,128]{3,2,1,0:T(1,128)S(1)} fusion(f32[32,32,128,1]{2,3,1,0:T(1,128)S(1)} %bitcast.145, f32[32,32,128]{2,1,0:T(8,128)S(1)} %dynamic-slice_bitcast_fusion.2, pred[32,128,128]{2,1,0:T(8,128)(4,1)S(1)} %compare_and_fusion.2), kind=kOutput, calls=%fused_computation.1.clone.2 | convolution fusion | flops 268435456 | bytes 2097152 | tf_op jit(solution)/shard_map/while/body/eval_jaxpr/rctj,rcj->rct/dot_general | solution.py:37
  241.3 0.9 constant_dynamic-update-slice_fusion.2
  242.2 1.1 constant_dynamic-slice_fusion.2
  243.3 0.7 compare_and_fusion.2
  244.0 110.7 %fusion.60 = f32[32,32,1,128]{3,2,1,0:T(1,128)S(1)} fusion(f32[32,32,128,1]{2,3,1,0:T(1,128)S(1)} %bitcast.145, f32[32,32,128]{2,1,0:T(8,128)S(1)} %dynamic-slice_bitcast_fusion.2, pred[32,128,128]{2,1,0:T(8,128)(4,1)S(1)} %compare_and_fusion.2), kind=kOutput, calls=%fused_computation.1.clone.2 | convolution fusion | flops 268435456 | bytes 2097152 | tf_op jit(solution)/shard_map/while/body/eval_jaxpr/rctj,rcj->rct/dot_general | solution.py:37
  354.7 0.9 constant_dynamic-update-slice_fusion.2
  355.6 1.1 constant_dynamic-slice_fusion.2
  356.7 0.7 compare_and_fusion.2
  357.4 110.7 %fusion.60 = f32[32,32,1,128]{3,2,1,0:T(1,128)S(1)} fusion(f32[32,32,128,1]{2,3,1,0:T(1,128)S(1)} %bitcast.145, f32[32,32,128]{2,1,0:T(8,128)S(1)} %dynamic-slice_bitcast_fusion.2, pred[32,128,128]{2,1,0:T(8,128)(4,1)S(1)} %compare_and_fusion.2), kind=kOutput, calls=%fused_computation.1.clone.2 | convolution fusion | flops 268435456 | bytes 2097152 | tf_op jit(solution)/shard_map/while/body/eval_jaxpr/rctj,rcj->rct/dot_general | solution.py:37
  468.1 0.9 constant_dynamic-update-slice_fusion.2
  469.0 1.1 constant_dynamic-slice_fusion.2
  470.1 0.7 compare_and_fusion.2
  470.9 110.7 %fusion.60 = f32[32,32,1,128]{3,2,1,0:T(1,128)S(1)} fusion(f32[32,32,128,1]{2,3,1,0:T(1,128)S(1)} %bitcast.145, f32[32,32,128]{2,1,0:T(8,128)S(1)} %dynamic-slice_bitcast_fusion.2, pred[32,128,128]{2,1,0:T(8,128)(4,1)S(1)} %compare_and_fusion.2), kind=kOutput, calls=%fused_computation.1.clone.2 | convolution fusion | flops 268435456 | bytes 2097152 | tf_op jit(solution)/shard_map/while/body/eval_jaxpr/rctj,rcj->rct/dot_general | solution.py:37
  581.5 0.8 constant_dynamic-update-slice_fusion.2
  582.4 2.0 copy.29
  584.4 0.0 copy-start.1
  584.4 0.0 copy-start
  584.4 1.5 copy-done.1
  585.9 1.9 slice_reduce_fusion.1
  587.8 0.0 copy-done
  587.8 1.9 slice_reduce_fusion
  590.4 0.0 copy-start.3
  590.4 2.3 multiply_add_fusion
  592.7 0.0 copy-done.3
  592.7 0.7 fusion.16
  593.9 65.6 %all_to_all.5 = f32[16,2,160,128]{3,2,1,0:T(8,128)S(1)} all-to-all(f32[16,2,160,128]{3,2,1,0:T(8,128)S(1)} %fusion.19), channel_id=1, replica_groups=mesh['seq'=16,'chan'=2] {'seq'}, dimensions={0} | all-to-all | bytes 5242880 | tf_op jit(solution)/shard_map/all_to_all | solution.py:85
  659.4 0.2 copy.31
  659.6 0.0 copy-start.4
  659.6 0.4 multiply_reduce_fusion
  660.0 5.0 psum.7
  665.0 0.0 copy-done.4
  665.0 1.5 fusion.18
  (64 shorter events, 1.3 us)
Async XLA Ops:
  6.6 0.8 copy-start.5
  10.6 1.7 copy-start.2
  584.4 1.5 copy-start.1
  584.4 3.4 copy-start
  590.4 2.3 copy-start.3
  659.6 5.3 copy-start.4
